TPU v7x, 32 devices: a whole 2x2x4 slice. The times are simulated.
32 devices in a mesh: gx: 4 (over x, core), gy: 2 (over y), gz: 4 (over z).
Axes of the slice: x: 2, y: 2, z: 4, core: 2. Of those that a mesh axis runs over, the one named last changes fastest.
Arguments:
- initial: float32 [64, 64, 512], P('gx', 'gy', 'gz'), may hold values from 0.5 to 2
- field_a: float32 [64, 64, 512], P('gx', 'gy', 'gz'), may hold values from -3 to 3
- field_b: float32 [64, 64, 512], P('gx', 'gy', 'gz'), may hold values from -3 to 3
- partner: float32 [3, 64, 64, 512], P(None, 'gx', 'gy', 'gz'), may hold values from 0.5 to 2
- store_a: float32 [64, 64, 512], P('gx', 'gy', 'gz'), may hold values from 0.2 to 1
- store_b: float32 [64, 64, 512], P('gx', 'gy', 'gz'), may hold values from 0.2 to 1
Outputs:
- second: float32 [64, 64, 512], P('gx', 'gy', 'gz')
- dens_a: float32 [64, 64, 512], P('gx', 'gy', 'gz')
- dens_b: float32 [64, 64, 512], P('gx', 'gy', 'gz')
- misfit: float32 [], replicated
All inputs are finite; a program needn't handle non-finite values.
Results may differ from a plain program's by a relative error of at most 0.00012.
Values sent between devices are 32-bit elements; how exact they have to be, the bound alone decides.
No kernel may reach another device: no remote copies, remote signals or barrier semaphores. Data moves between devices by JAX's collectives and lax.ppermute only.
A program may use at most 64 MiB of HBM per device.

v0:
```python
import math

import jax
import jax.numpy as jnp
from jax import lax
from jax.sharding import PartitionSpec as P

contour_step = 0.25
coupling_value = 0.25 * 4096.0 / 6.0
highest = lax.Precision.HIGHEST


def line_rate():
    small_t = 0.5 / coupling_value
    return (coupling_value, math.log(1.0 + small_t + math.sqrt(small_t * (2.0 + small_t))))


def green_scale(line_total):
    coupling, decay_rate = line_rate()
    return 1.0 / (
        2.0 * coupling * math.sinh(decay_rate) * (1.0 - math.exp(-decay_rate * line_total))
    )


def stepping_table(size_rows, line_total):
    decay_rate = line_rate()[1]
    position = jnp.arange(size_rows, dtype=jnp.float32)
    distance = jnp.abs(position[:, None] - position[None, :])
    green = green_scale(line_total) * (
        jnp.exp(-decay_rate * distance) + jnp.exp(-decay_rate * (line_total - distance))
    )
    return 2.0 * green - jnp.eye(size_rows, dtype=jnp.float32)


def along(matrix, values, line_dim):
    if line_dim == 0:
        return jnp.einsum("ij,jbc->ibc", matrix, values, precision=highest)
    if line_dim == 1:
        return jnp.einsum("ij,ajc->aic", matrix, values, precision=highest)
    return jnp.einsum("ij,abj->abi", matrix, values, precision=highest)


def block_parts(values, line_dim, line_total):
    cells = values.shape[line_dim]
    decay_rate = line_rate()[1]
    position = jnp.arange(cells, dtype=jnp.float32)
    weights = jnp.stack([jnp.exp(decay_rate * position), jnp.exp(-decay_rate * position)], axis=0)
    inside = along(stepping_table(cells, line_total), values, line_dim)
    return (inside, along(weights, values, line_dim))


def block_finish(inside, coeffs, line_dim, cells, count):
    decay_rate = line_rate()[1]
    position = jnp.arange(cells, dtype=jnp.float32)
    basis = jnp.stack([jnp.exp(-decay_rate * position), jnp.exp(decay_rate * position)], axis=1)
    return inside + 2.0 * green_scale(cells * count) * along(basis, coeffs, line_dim)


def spread_matrix(device_index, count, cells):
    decay_rate = line_rate()[1]
    blocks = jnp.arange(count, dtype=jnp.int32)
    lag_low = jnp.mod(device_index - blocks, count).astype(jnp.float32)
    lag_high = jnp.mod(blocks - device_index, count).astype(jnp.float32)
    weight_low = jnp.where(blocks == device_index, 0.0, jnp.exp(-decay_rate * cells * lag_low))
    weight_high = jnp.where(blocks == device_index, 0.0, jnp.exp(-decay_rate * cells * lag_high))
    nothing = jnp.zeros((count,), jnp.float32)
    row_plus = jnp.stack([weight_low, nothing], axis=1).reshape(2 * count)
    row_minus = jnp.stack([nothing, weight_high], axis=1).reshape(2 * count)
    return jnp.stack([row_plus, row_minus], axis=0)


def sweep_x(values):
    count = lax.axis_size("gx")
    cells = values.shape[0]
    inside, moments = block_parts(values, 0, cells * count)
    gathered = lax.all_gather(moments, "gx", axis=0, tiled=True)
    coeffs = along(spread_matrix(lax.axis_index("gx"), count, cells), gathered, 0)
    return block_finish(inside, coeffs, 0, cells, count)


def sweep_y(values):
    count = lax.axis_size("gy")
    cells = values.shape[1]
    inside, moments = block_parts(values, 1, cells * count)
    gathered = lax.all_gather(moments, "gy", axis=1, tiled=True)
    coeffs = along(spread_matrix(lax.axis_index("gy"), count, cells), gathered, 1)
    return block_finish(inside, coeffs, 1, cells, count)


def sweep_z(values):
    count = lax.axis_size("gz")
    cells = values.shape[2]
    inside, moments = block_parts(values, 2, cells * count)
    gathered = lax.all_gather(moments, "gz", axis=2, tiled=True)
    coeffs = along(spread_matrix(lax.axis_index("gz"), count, cells), gathered, 2)
    return block_finish(inside, coeffs, 2, cells, count)


def advance(propagator, field):
    factor = jnp.exp(-0.5 * contour_step * field)
    values = sweep_z(sweep_y(sweep_x(factor * propagator)))
    return factor * values


def shards(initial, field_a, field_b, partner, store_a, store_b):
    first = advance(initial, field_a)
    second = advance(first, field_b)
    halfstep = 0.5 * contour_step
    raw_a = store_a + halfstep * (initial * partner[0] + first * partner[1])
    raw_b = store_b + halfstep * (first * partner[1] + second * partner[2])
    cell_total = initial.size * lax.axis_size("gx") * lax.axis_size("gy") * lax.axis_size("gz")
    norm_sum = lax.psum(jnp.sum(initial * partner[0]), ("gx", "gy", "gz"))
    weight = norm_sum / cell_total
    dens_a = raw_a / weight
    dens_b = raw_b / weight
    misfit = lax.psum(jnp.sum(jnp.square(dens_a + dens_b - 1.0)), ("gx", "gy", "gz")) / cell_total
    return (second, dens_a, dens_b, misfit)


def solution(mesh):
    return jax.shard_map(
        shards,
        mesh=mesh,
        in_specs=(
            P("gx", "gy", "gz"),
            P("gx", "gy", "gz"),
            P("gx", "gy", "gz"),
            P(None, "gx", "gy", "gz"),
            P("gx", "gy", "gz"),
            P("gx", "gy", "gz"),
        ),
        out_specs=(P("gx", "gy", "gz"), P("gx", "gy", "gz"), P("gx", "gy", "gz"), P()),
        check_vma=False,
    )
```

profile of v0, /device:TPU:0, one launch (start us, length us, event | category | flops | bytes accessed | tf_op | source)
XLA Modules:
  0.0 146.9 jit_solution(9439656562878156025)
XLA Ops:
  0.8 0.1 stack_reshape.26
  0.9 0.1 stack.37
  0.9 0.1 stack_reshape.27
  1.0 0.1 stack_reshape.24
  1.1 0.1 stack.32
  1.2 0.1 stack_reshape.25
  1.3 0.1 stack_reshape.28
  1.4 0.1 stack.42
  1.5 0.1 stack_reshape.29
  1.6 1.8 %fusion.34 = (f32[]{:T(128)}, f32[16,32,128]{2,1,0:T(8,128)S(1)}) fusion(f32[16,32,128]{2,1,0:T(8,128)} %param.6, f32[3,16,32,128]{3,2,1,0:T(8,128)} %param.9, f32[16,32,128]{2,1,0:T(8,128)} %param.7), kind=kLoop, calls=%fused_computation.51 | loop fusion | flops 262143 | bytes 1048580 | tf_op jit(solution)/shard_map/reduce_sum | solution.py:112
  3.4 42.2 %psum.14 = f32[]{:T(128)} all-reduce(f32[]{:T(128)} %get-tuple-element.7), channel_id=1, replica_groups=mesh['gx'=4,'gy'=2,'gz'=4] {'gx','gy','gz'}, use_global_device_ids=true, to_apply=%region_1.2 | all-reduce | flops 1 | bytes 8 | tf_op jit(solution)/shard_map/psum | solution.py:112
  46.2 0.4 fusion.24
  46.6 0.5 fusion.26
  47.1 5.8 %all_gather.18 = f32[8,32,128]{2,1,0:T(8,128)S(1)} all-gather(f32[2,32,128]{2,1,0:T(8,128)S(1)} %copy.20), channel_id=1, replica_groups=mesh['gx'=4,'gy'=2,'gz'=4] {'gx'}, dimensions={0}, use_global_device_ids=true | all-gather | bytes 163840 | tf_op jit(solution)/shard_map/all_gather | solution.py:76
  52.9 0.3 fusion.32
  53.2 0.5 fusion.5
  53.7 0.3 convolution_bitcast_fusion.3
  54.0 0.4 fusion.22
  54.5 4.4 %all_gather.19 = f32[16,4,128]{2,0,1:T(8,128)S(1)} all-gather(f32[16,2,128]{2,0,1:T(8,128)S(1)} %copy.24), channel_id=1, replica_groups=mesh['gx'=4,'gy'=2,'gz'=4] {'gy'}, dimensions={1}, use_global_device_ids=true | all-gather | bytes 49152 | tf_op jit(solution)/shard_map/all_gather | solution.py:85
  58.9 0.2 convolution_bitcast_fusion.1
  59.1 0.4 fusion.8
  59.5 1.1 fusion.98
  60.6 0.0 copy-start
  60.6 0.0 copy-start.2
  60.6 0.4 fusion.37
  61.1 13.1 %all_gather.20 = f32[16,32,8]{1,0,2:T(8,128)S(1)} all-gather(f32[16,32,2]{1,0,2:T(8,128)S(1)} %copy.26), channel_id=1, replica_groups=mesh['gx'=4,'gy'=2,'gz'=4] {'gz'}, dimensions={2}, use_global_device_ids=true | all-gather | bytes 20480 | tf_op jit(solution)/shard_map/all_gather | solution.py:94
  74.2 0.2 fusion.41
  74.4 0.0 copy-done
  74.4 0.0 copy-done.2
  74.4 0.6 fusion.28
  75.1 0.4 fusion.17
  75.5 0.5 fusion.19
  76.0 5.4 %all_gather.21 = f32[8,32,128]{2,1,0:T(8,128)S(1)} all-gather(f32[2,32,128]{2,1,0:T(8,128)S(1)} %copy.30), channel_id=1, replica_groups=mesh['gx'=4,'gy'=2,'gz'=4] {'gx'}, dimensions={0}, use_global_device_ids=true | all-gather | bytes 163840 | tf_op jit(solution)/shard_map/all_gather | solution.py:76
  81.4 0.3 fusion.30
  81.7 0.5 fusion.2
  82.2 0.3 convolution_bitcast_fusion.2
  82.5 0.4 fusion.15
  83.0 4.4 %all_gather.22 = f32[16,4,128]{2,0,1:T(8,128)S(1)} all-gather(f32[16,2,128]{2,0,1:T(8,128)S(1)} %copy.34), channel_id=1, replica_groups=mesh['gx'=4,'gy'=2,'gz'=4] {'gy'}, dimensions={1}, use_global_device_ids=true | all-gather | bytes 49152 | tf_op jit(solution)/shard_map/all_gather | solution.py:85
  87.4 0.2 convolution_bitcast_fusion
  87.6 0.4 fusion.9
  88.0 0.0 copy-start.4
  88.0 1.1 fusion.97
  89.1 0.0 copy-start.1
  89.1 0.0 copy-start.3
  89.1 0.4 fusion.35
  89.6 13.1 %all_gather.23 = f32[16,32,8]{1,0,2:T(8,128)S(1)} all-gather(f32[16,32,2]{1,0,2:T(8,128)S(1)} %copy.36), channel_id=1, replica_groups=mesh['gx'=4,'gy'=2,'gz'=4] {'gz'}, dimensions={2}, use_global_device_ids=true | all-gather | bytes 20480 | tf_op jit(solution)/shard_map/all_gather | solution.py:94
  102.7 0.2 fusion.39
  102.9 0.0 copy-done.4
  102.9 0.0 copy-done.1
  102.9 0.0 copy-done.3
  102.9 3.3 %multiply_reduce_fusion = (f32[]{:T(128)}, f32[16,32,128]{2,1,0:T(8,128)}, f32[16,32,128]{2,1,0:T(8,128)}, f32[16,32,128]{2,1,0:T(8,128)}) fusion(f32[]{:T(128)S(6)} %div.16, f32[16,32,128]{2,1,0:T(8,128)S(1)} %copy-done.3, f32[3,16,32,128]{3,2,1,0:T(8,128)} %param.9, f32[16,32,128]{2,1,0:T(8,128)S(1)} %get-tuple-element.10, ...), kind=kOutput, calls=%fused_computation.27 | convolution fusion | flops 2818303 | bytes 3150856 | tf_op jit(solution)/shard_map/ij,abj->abi/dot_general | solution.py:40
  106.2 38.9 %psum.15 = f32[]{:T(128)} all-reduce(f32[]{:T(128)} %get-tuple-element.4), channel_id=1, replica_groups=mesh['gx'=4,'gy'=2,'gz'=4] {'gx','gy','gz'}, use_global_device_ids=true, to_apply=%region_3.4 | all-reduce | flops 1 | bytes 8 | tf_op jit(solution)/shard_map/psum | solution.py:116
  (18 shorter events, 0.2 us)
Async XLA Ops:
  60.6 13.8 %copy-start = (f32[16,32,128]{2,1,0:T(8,128)S(1)}, f32[16,32,128]{2,1,0:T(8,128)}, u32[]{:S(2)}) copy-start(f32[16,32,128]{2,1,0:T(8,128)} %param.7) | copy-start | bytes 786436
  60.6 13.8 %copy-start.2 = (f32[16,32,128]{2,1,0:T(8,128)S(1)}, f32[16,32,128]{2,1,0:T(8,128)}, u32[]{:S(2)}) copy-start(f32[16,32,128]{2,1,0:T(8,128)} %param.8) | copy-start | bytes 786436
  88.0 14.9 %copy-start.4 = (f32[16,32,128]{2,1,0:T(8,128)S(1)}, f32[16,32,128]{2,1,0:T(8,128)}, u32[]{:S(2)}) copy-start(f32[16,32,128]{2,1,0:T(8,128)} %param.10) | copy-start | bytes 786436
  89.1 13.8 %copy-start.1 = (f32[16,32,128]{2,1,0:T(8,128)S(1)}, f32[16,32,128]{2,1,0:T(8,128)}, u32[]{:S(2)}) copy-start(f32[16,32,128]{2,1,0:T(8,128)} %param.6) | copy-start | bytes 786436
  89.1 13.8 %copy-start.3 = (f32[16,32,128]{2,1,0:T(8,128)S(1)}, f32[16,32,128]{2,1,0:T(8,128)}, u32[]{:S(2)}) copy-start(f32[16,32,128]{2,1,0:T(8,128)} %param.11) | copy-start | bytes 786436
where the time goes:
time: 147 us
  blocking collectives  127 us (86%)
  matrix products  13.4 us (9%)
  between operations  3.39 us (2%)
  other arithmetic  1.92 us (1%)
    psum x1, blocking collectives, shards(): norm_sum = lax.psum(jnp.sum(initial * partner[0]), ('gx', 'gy', 'gz'))  42.2 us
    psum x1, blocking collectives, shards(): lax.psum(jnp.sum(jnp.square(dens_a + dens_b - 1.0)), ('gx', 'gy', 'gz'))  38.9 us
    all_gather x2, blocking collectives, sweep_z(): gathered = lax.all_gather(moments, 'gz', axis=2, tiled=True)  26.3 us
    all_gather x2, blocking collectives, sweep_x(): gathered = lax.all_gather(moments, 'gx', axis=0, tiled=True)  11.2 us
    all_gather x2, blocking collectives, sweep_y(): gathered = lax.all_gather(moments, 'gy', axis=1, tiled=True)  8.83 us
    dot_general x8, matrix products, along(): return jnp.einsum('ij,abj->abi', matrix, values, precision=highest)  7.36 us
    dot_general x8, matrix products, along(): return jnp.einsum('ij,jbc->ibc', matrix, values, precision=highest)  3.31 us

commit v1 on v0

--- a/solution.py
+++ b/solution.py
@@ -69,6 +69,35 @@
     return jnp.stack([row_plus, row_minus], axis=0)
 
 
+def swap(values, axis, bit):
+    count = lax.axis_size(axis)
+    return lax.ppermute(values, axis, [(i, i ^ bit) for i in range(count)])
+
+
+def bits_of(axis):
+    count = lax.axis_size(axis)
+    if count & (count - 1):
+        raise ValueError("axis size")
+    return [1 << k for k in range(count.bit_length() - 1)]
+
+
+def swap_sum(value):
+    for axis in ("gx", "gy", "gz"):
+        for bit in bits_of(axis):
+            value = value + swap(value, axis, bit)
+    return value
+
+
+def swap_gather(values, axis, dim):
+    for bit in bits_of(axis):
+        other = swap(values, axis, bit)
+        upper = (lax.axis_index(axis) & bit) != 0
+        values = jnp.concatenate(
+            [jnp.where(upper, other, values), jnp.where(upper, values, other)], axis=dim
+        )
+    return values
+
+
 def sweep_x(values):
     count = lax.axis_size("gx")
     cells = values.shape[0]
@@ -91,7 +120,7 @@
     count = lax.axis_size("gz")
     cells = values.shape[2]
     inside, moments = block_parts(values, 2, cells * count)
-    gathered = lax.all_gather(moments, "gz", axis=2, tiled=True)
+    gathered = swap_gather(moments, "gz", 2)
     coeffs = along(spread_matrix(lax.axis_index("gz"), count, cells), gathered, 2)
     return block_finish(inside, coeffs, 2, cells, count)
 
@@ -109,11 +138,11 @@
     raw_a = store_a + halfstep * (initial * partner[0] + first * partner[1])
     raw_b = store_b + halfstep * (first * partner[1] + second * partner[2])
     cell_total = initial.size * lax.axis_size("gx") * lax.axis_size("gy") * lax.axis_size("gz")
-    norm_sum = lax.psum(jnp.sum(initial * partner[0]), ("gx", "gy", "gz"))
+    norm_sum = swap_sum(jnp.sum(initial * partner[0]))
     weight = norm_sum / cell_total
     dens_a = raw_a / weight
     dens_b = raw_b / weight
-    misfit = lax.psum(jnp.sum(jnp.square(dens_a + dens_b - 1.0)), ("gx", "gy", "gz")) / cell_total
+    misfit = swap_sum(jnp.sum(jnp.square(dens_a + dens_b - 1.0))) / cell_total
     return (second, dens_a, dens_b, misfit)
 
 

time: 147 us -> 95.9 us (0.65)
  blocking collectives: 127 us -> 20.7 us
  starting transfers between devices: 0 us -> 33.1 us
  waiting for transfers between devices: 0 us -> 15.8 us
  between operations: 3.39 us -> 9.8 us
    psum x2 -> x0, blocking collectives: 81.1 us -> none  [the longest x1 42.2 us: shards(): norm_sum = lax.psum(jnp.sum(initial * partner[0]), ('gx', 'gy', 'gz'))]
    ppermute x0 -> x14, starting transfers between devices: none -> 33.1 us  [swap(): return lax.ppermute(values, axis, [(i, i ^ bit) for i in range(count)])]
    all_gather x2 -> x0, blocking collectives: 26.3 us -> none  [sweep_z(): gathered = lax.all_gather(moments, 'gz', axis=2, tiled=True)]
    ppermute x0 -> x14, waiting for transfers between devices: none -> 15.8 us  [swap(): return lax.ppermute(values, axis, [(i, i ^ bit) for i in range(count)])]
  transfers between devices with their start and end apart: 0 -> 14, of which waited for: 0 -> 13; matrix products, arithmetic and copies ran while one was open for 0% -> 1% of each run, Pallas kernels for 0% -> 0%
where the time goes in v1:
time: 95.9 us; the launch traced here: 95.6 us
  starting transfers between devices  33.1 us (35%)
  blocking collectives  20.7 us (22%)
  waiting for transfers between devices  15.8 us (16%)
  matrix products  13.4 us (14%)
  between operations  9.8 us (10%)
  other arithmetic  2.03 us (2%)
    ppermute x14, starting transfers between devices, swap(): return lax.ppermute(values, axis, [(i, i ^ bit) for i in range(count)])  33.1 us
    ppermute x14, waiting for transfers between devices, swap(): return lax.ppermute(values, axis, [(i, i ^ bit) for i in range(count)])  15.8 us
    all_gather x2, blocking collectives, sweep_x(): gathered = lax.all_gather(moments, 'gx', axis=0, tiled=True)  11.9 us
    all_gather x2, blocking collectives, sweep_y(): gathered = lax.all_gather(moments, 'gy', axis=1, tiled=True)  8.81 us
    dot_general x8, matrix products, along(): return jnp.einsum('ij,abj->abi', matrix, values, precision=highest)  7.32 us
    dot_general x8, matrix products, along(): return jnp.einsum('ij,jbc->ibc', matrix, values, precision=highest)  3.32 us
    dot_general x8, matrix products, along(): return jnp.einsum('ij,ajc->aic', matrix, values, precision=highest)  2.71 us
  transfers between devices with their start and end apart: 14, of which 13 were waited for; matrix products, arithmetic and copies ran while one was open for 1% of the time, Pallas kernels for 0%

profile of v1, /device:TPU:0, one launch (start us, length us, event | category | flops | bytes accessed | tf_op | source)
XLA Modules:
  0.0 95.6 jit_solution(10101829311457688506)
XLA Ops:
  0.8 0.1 stack_reshape.26
  0.8 0.1 stack.37
  0.9 0.1 stack_reshape.27
  1.0 0.1 stack_reshape.24
  1.1 0.1 stack.32
  1.2 0.1 stack_reshape.25
  1.3 1.8 %fusion.34 = (f32[]{:T(128)}, f32[16,32,128]{2,1,0:T(8,128)S(1)}) fusion(f32[16,32,128]{2,1,0:T(8,128)} %param.6, f32[3,16,32,128]{3,2,1,0:T(8,128)} %param.9, f32[16,32,128]{2,1,0:T(8,128)} %param.7), kind=kLoop, calls=%fused_computation.51 | loop fusion | flops 262143 | bytes 1048580 | tf_op jit(solution)/shard_map/reduce_sum | solution.py:141
  3.1 0.5 fusion.26
  3.6 0.4 fusion.24
  4.0 6.5 %all_gather.12 = f32[8,32,128]{2,1,0:T(8,128)S(1)} all-gather(f32[2,32,128]{2,1,0:T(8,128)S(1)} %copy.20), channel_id=1, replica_groups=mesh['gx'=4,'gy'=2,'gz'=4] {'gx'}, dimensions={0}, use_global_device_ids=true | all-gather | bytes 163840 | tf_op jit(solution)/shard_map/all_gather | solution.py:105
  10.5 0.3 fusion.32
  10.8 0.5 fusion.5
  11.3 0.4 fusion.22
  11.7 0.3 convolution_bitcast_fusion.3
  12.0 4.4 %all_gather.13 = f32[16,4,128]{2,0,1:T(8,128)S(1)} all-gather(f32[16,2,128]{2,0,1:T(8,128)S(1)} %copy.24), channel_id=1, replica_groups=mesh['gx'=4,'gy'=2,'gz'=4] {'gy'}, dimensions={1}, use_global_device_ids=true | all-gather | bytes 49152 | tf_op jit(solution)/shard_map/all_gather | solution.py:114
  16.5 0.2 convolution_bitcast_fusion.1
  16.7 0.4 fusion.8
  17.1 1.1 %fusion.102 = f32[16,32,2]{1,2,0:T(2,128)S(1)} fusion(f32[16,32,128]{2,1,0:T(8,128)S(1)} %fusion.8, f32[1,128]{1,0:T(1,128)S(1)} %get-tuple-element.32, f32[1,128]{1,0:T(1,128)S(1)} %get-tuple-element.33), kind=kOutput, calls=%fused_computation.177 | convolution fusion | flops 1573120 | bytes 267264 | tf_op jit(solution)/shard_map/ij,abj->abi/dot_general | solution.py:40
  18.2 2.0 %collective-permute-start = (f32[16,32,2]{1,2,0:T(2,128)S(1)}, f32[16,32,2]{1,2,0:T(2,128)S(1)}, u32[]{:S(2)}, u32[]{:S(2)}) collective-permute-start(f32[16,32,2]{1,2,0:T(2,128)S(1)} %fusion.102), channel_id=1, source_target_pairs={{0,1},{1,0},{2,3},{3,2},{4,5},{5,4},{6,7},{7,6},{8,9},{9,8},{10,11... | collective-permute-start | bytes 12296 | tf_op jit(solution)/shard_map/ppermute | solution.py:74
  20.2 0.4 fusion.45
  20.6 0.0 copy-start
  20.6 1.3 %collective-permute-done = f32[16,32,2]{1,2,0:T(2,128)S(1)} collective-permute-done((f32[16,32,2]{1,2,0:T(2,128)S(1)}, f32[16,32,2]{1,2,0:T(2,128)S(1)}, u32[]{:S(2)}, u32[]{:S(2)}) %collective-permute-start) | collective-permute-done | bytes 4128 | tf_op jit(solution)/shard_map/ppermute | solution.py:74
  22.0 3.0 %collective-permute-start.1 = (f32[16,32,4]{1,2,0:T(4,128)S(1)}, f32[16,32,4]{1,2,0:T(4,128)S(1)}, u32[]{:S(2)}, u32[]{:S(2)}) collective-permute-start(f32[16,32,4]{1,2,0:T(4,128)S(1)} %pad_maximum_fusion), channel_id=1, source_target_pairs={{0,2},{1,3},{2,0},{3,1},{4,6},{5,7},{6,4},{7,5},{8,10},{9,11},{10,... | collective-permute-start | bytes 24584 | tf_op jit(solution)/shard_map/ppermute | solution.py:74
  25.0 0.1 stack_reshape.28
  25.1 0.1 stack.42
  25.2 0.1 stack_reshape.29
  25.3 1.6 %collective-permute-done.1 = f32[16,32,4]{1,2,0:T(4,128)S(1)} collective-permute-done((f32[16,32,4]{1,2,0:T(4,128)S(1)}, f32[16,32,4]{1,2,0:T(4,128)S(1)}, u32[]{:S(2)}, u32[]{:S(2)}) %collective-permute-start.1) | collective-permute-done | bytes 8224 | tf_op jit(solution)/shard_map/ppermute | solution.py:74
  26.9 0.2 fusion.35
  27.2 0.6 fusion.28
  27.8 0.4 fusion.17
  28.2 0.5 fusion.19
  28.7 5.4 %all_gather.14 = f32[8,32,128]{2,1,0:T(8,128)S(1)} all-gather(f32[2,32,128]{2,1,0:T(8,128)S(1)} %copy.28), channel_id=1, replica_groups=mesh['gx'=4,'gy'=2,'gz'=4] {'gx'}, dimensions={0}, use_global_device_ids=true | all-gather | bytes 163840 | tf_op jit(solution)/shard_map/all_gather | solution.py:105
  34.1 0.3 fusion.30
  34.4 0.5 fusion.2
  34.9 0.3 convolution_bitcast_fusion.2
  35.3 0.4 fusion.15
  35.7 4.4 %all_gather.15 = f32[16,4,128]{2,0,1:T(8,128)S(1)} all-gather(f32[16,2,128]{2,0,1:T(8,128)S(1)} %copy.32), channel_id=1, replica_groups=mesh['gx'=4,'gy'=2,'gz'=4] {'gy'}, dimensions={1}, use_global_device_ids=true | all-gather | bytes 49152 | tf_op jit(solution)/shard_map/all_gather | solution.py:114
  40.1 0.2 convolution_bitcast_fusion
  40.3 0.4 fusion.9
  40.7 1.1 %fusion.101 = f32[16,32,2]{1,2,0:T(2,128)S(1)} fusion(f32[16,32,128]{2,1,0:T(8,128)S(1)} %fusion.9, f32[1,128]{1,0:T(1,128)S(1)} %get-tuple-element.32, f32[1,128]{1,0:T(1,128)S(1)} %get-tuple-element.33), kind=kOutput, calls=%fused_computation.176 | convolution fusion | flops 1573120 | bytes 267264 | tf_op jit(solution)/shard_map/ij,abj->abi/dot_general | solution.py:40
  41.8 1.9 %collective-permute-start.2 = (f32[16,32,2]{1,2,0:T(2,128)S(1)}, f32[16,32,2]{1,2,0:T(2,128)S(1)}, u32[]{:S(2)}, u32[]{:S(2)}) collective-permute-start(f32[16,32,2]{1,2,0:T(2,128)S(1)} %fusion.101), channel_id=1, source_target_pairs={{0,1},{1,0},{2,3},{3,2},{4,5},{5,4},{6,7},{7,6},{8,9},{9,8},{10,11... | collective-permute-start | bytes 12296 | tf_op jit(solution)/shard_map/ppermute | solution.py:74
  43.8 1.4 %collective-permute-done.4 = f32[]{:T(128)} collective-permute-done((f32[]{:T(128)}, f32[]{:T(128)}, u32[]{:S(2)}, u32[]{:S(2)}) %collective-permute-start.4) | collective-permute-done | bytes 36 | tf_op jit(solution)/shard_map/ppermute | solution.py:74
  46.5 2.9 %collective-permute-start.5 = (f32[]{:T(128)}, f32[]{:T(128)}, u32[]{:S(2)}, u32[]{:S(2)}) collective-permute-start(f32[]{:T(128)} %add.201), channel_id=1, source_target_pairs={{0,16},{8,24},{16,0},{24,8},{1,17},{9,25},{17,1},{25,9},{2,18},{10... | collective-permute-start | bytes 20 | tf_op jit(solution)/shard_map/ppermute | solution.py:74
  49.3 0.9 collective-permute-done.5
  50.9 2.9 %collective-permute-start.6 = (f32[]{:T(128)}, f32[]{:T(128)}, u32[]{:S(2)}, u32[]{:S(2)}) collective-permute-start(f32[]{:T(128)} %add.202), channel_id=1, source_target_pairs={{0,4},{4,0},{1,5},{5,1},{2,6},{6,2},{3,7},{7,3},{8,12},{12,8},{9,1... | collective-permute-start | bytes 20 | tf_op jit(solution)/shard_map/ppermute | solution.py:74
  53.7 0.8 collective-permute-done.6
  55.2 1.5 %collective-permute-start.7 = (f32[]{:T(128)}, f32[]{:T(128)}, u32[]{:S(2)}, u32[]{:S(2)}) collective-permute-start(f32[]{:T(128)} %add.203), channel_id=1, source_target_pairs={{0,1},{1,0},{2,3},{3,2},{4,5},{5,4},{6,7},{7,6},{8,9},{9,8},{10,11... | collective-permute-start | bytes 20 | tf_op jit(solution)/shard_map/ppermute | solution.py:74
  56.7 2.3 %collective-permute-done.7 = f32[]{:T(128)} collective-permute-done((f32[]{:T(128)}, f32[]{:T(128)}, u32[]{:S(2)}, u32[]{:S(2)}) %collective-permute-start.7) | collective-permute-done | bytes 36 | tf_op jit(solution)/shard_map/ppermute | solution.py:74
  59.6 4.2 %collective-permute-start.8 = (f32[]{:T(128)}, f32[]{:T(128)}, u32[]{:S(2)}, u32[]{:S(2)}) collective-permute-start(f32[]{:T(128)} %add.204), channel_id=1, source_target_pairs={{0,2},{1,3},{2,0},{3,1},{4,6},{5,7},{6,4},{7,5},{8,10},{9,11},{10,... | collective-permute-start | bytes 20 | tf_op jit(solution)/shard_map/ppermute | solution.py:74
  63.8 0.5 collective-permute-done.8
  65.0 2.9 %collective-permute-start.3 = (f32[16,32,4]{1,2,0:T(4,128)S(1)}, f32[16,32,4]{1,2,0:T(4,128)S(1)}, u32[]{:S(2)}, u32[]{:S(2)}) collective-permute-start(f32[16,32,4]{1,2,0:T(4,128)S(1)} %pad_maximum_fusion.1), channel_id=1, source_target_pairs={{0,2},{1,3},{2,0},{3,1},{4,6},{5,7},{6,4},{7,5},{8,10},{9,11},{10,... | collective-permute-start | bytes 24584 | tf_op jit(solution)/shard_map/ppermute | solution.py:74
  67.9 0.4 fusion.43
  68.3 1.6 %collective-permute-done.3 = f32[16,32,4]{1,2,0:T(4,128)S(1)} collective-permute-done((f32[16,32,4]{1,2,0:T(4,128)S(1)}, f32[16,32,4]{1,2,0:T(4,128)S(1)}, u32[]{:S(2)}, u32[]{:S(2)}) %collective-permute-start.3) | collective-permute-done | bytes 8224 | tf_op jit(solution)/shard_map/ppermute | solution.py:74
  69.9 0.2 fusion.39
  70.1 3.2 %multiply_reduce_fusion = (f32[]{:T(128)}, f32[16,32,128]{2,1,0:T(8,128)}, f32[16,32,128]{2,1,0:T(8,128)}, f32[16,32,128]{2,1,0:T(8,128)}) fusion(f32[]{:T(128)S(6)} %div.16, f32[16,32,128]{2,1,0:T(8,128)S(1)} %copy-done.3, f32[3,16,32,128]{3,2,1,0:T(8,128)} %param.9, f32[16,32,128]{2,1,0:T(8,128)S(1)} %get-tuple-element.18, ...), kind=kOutput, calls=%fused_computation.27 | convolution fusion | flops 2818303 | bytes 3150856 | tf_op jit(solution)/shard_map/ij,abj->abi/dot_general | solution.py:40
  73.4 1.4 %collective-permute-done.9 = f32[]{:T(128)} collective-permute-done((f32[]{:T(128)}, f32[]{:T(128)}, u32[]{:S(2)}, u32[]{:S(2)}) %collective-permute-start.9) | collective-permute-done | bytes 36 | tf_op jit(solution)/shard_map/ppermute | solution.py:74
  76.1 3.1 %collective-permute-start.10 = (f32[]{:T(128)}, f32[]{:T(128)}, u32[]{:S(2)}, u32[]{:S(2)}) collective-permute-start(f32[]{:T(128)} %add.209), channel_id=1, source_target_pairs={{0,16},{8,24},{16,0},{24,8},{1,17},{9,25},{17,1},{25,9},{2,18},{10... | collective-permute-start | bytes 20 | tf_op jit(solution)/shard_map/ppermute | solution.py:74
  79.2 0.6 collective-permute-done.10
  80.5 3.1 %collective-permute-start.11 = (f32[]{:T(128)}, f32[]{:T(128)}, u32[]{:S(2)}, u32[]{:S(2)}) collective-permute-start(f32[]{:T(128)} %add.210), channel_id=1, source_target_pairs={{0,4},{4,0},{1,5},{5,1},{2,6},{6,2},{3,7},{7,3},{8,12},{12,8},{9,1... | collective-permute-start | bytes 20 | tf_op jit(solution)/shard_map/ppermute | solution.py:74
  83.6 0.6 collective-permute-done.11
  84.8 1.5 %collective-permute-start.12 = (f32[]{:T(128)}, f32[]{:T(128)}, u32[]{:S(2)}, u32[]{:S(2)}) collective-permute-start(f32[]{:T(128)} %add.211), channel_id=1, source_target_pairs={{0,1},{1,0},{2,3},{3,2},{4,5},{5,4},{6,7},{7,6},{8,9},{9,8},{10,11... | collective-permute-start | bytes 20 | tf_op jit(solution)/shard_map/ppermute | solution.py:74
  86.3 2.2 %collective-permute-done.12 = f32[]{:T(128)} collective-permute-done((f32[]{:T(128)}, f32[]{:T(128)}, u32[]{:S(2)}, u32[]{:S(2)}) %collective-permute-start.12) | collective-permute-done | bytes 36 | tf_op jit(solution)/shard_map/ppermute | solution.py:74
  89.2 4.2 %collective-permute-start.13 = (f32[]{:T(128)}, f32[]{:T(128)}, u32[]{:S(2)}, u32[]{:S(2)}) collective-permute-start(f32[]{:T(128)} %add.212), channel_id=1, source_target_pairs={{0,2},{1,3},{2,0},{3,1},{4,6},{5,7},{6,4},{7,5},{8,10},{9,11},{10,... | collective-permute-start | bytes 20 | tf_op jit(solution)/shard_map/ppermute | solution.py:74
  93.4 0.5 collective-permute-done.13
  (34 shorter events, 0.3 us)
Async XLA Ops:
  18.2 3.8 %collective-permute-start = (f32[16,32,2]{1,2,0:T(2,128)S(1)}, f32[16,32,2]{1,2,0:T(2,128)S(1)}, u32[]{:S(2)}, u32[]{:S(2)}) collective-permute-start(f32[16,32,2]{1,2,0:T(2,128)S(1)} %fusion.102), channel_id=1, source_target_pairs={{0,1},{1,0},{2,3},{3,2},{4,5},{5,4},{6,7},{7,6},{8,9},{9,8},{10,11... | collective-permute-start | bytes 12296 | tf_op jit(solution)/shard_map/ppermute | solution.py:74
  20.2 7.0 %copy-start.2 = (f32[16,32,128]{2,1,0:T(8,128)S(1)}, f32[16,32,128]{2,1,0:T(8,128)}, u32[]{:S(2)}) copy-start(f32[16,32,128]{2,1,0:T(8,128)} %param.8) | copy-start | bytes 786436
  20.6 6.6 %copy-start = (f32[16,32,128]{2,1,0:T(8,128)S(1)}, f32[16,32,128]{2,1,0:T(8,128)}, u32[]{:S(2)}) copy-start(f32[16,32,128]{2,1,0:T(8,128)} %param.7) | copy-start | bytes 786436
  22.0 4.9 %collective-permute-start.1 = (f32[16,32,4]{1,2,0:T(4,128)S(1)}, f32[16,32,4]{1,2,0:T(4,128)S(1)}, u32[]{:S(2)}, u32[]{:S(2)}) collective-permute-start(f32[16,32,4]{1,2,0:T(4,128)S(1)} %pad_maximum_fusion), channel_id=1, source_target_pairs={{0,2},{1,3},{2,0},{3,1},{4,6},{5,7},{6,4},{7,5},{8,10},{9,11},{10,... | collective-permute-start | bytes 24584 | tf_op jit(solution)/shard_map/ppermute | solution.py:74
  41.8 23.0 %collective-permute-start.2 = (f32[16,32,2]{1,2,0:T(2,128)S(1)}, f32[16,32,2]{1,2,0:T(2,128)S(1)}, u32[]{:S(2)}, u32[]{:S(2)}) collective-permute-start(f32[16,32,2]{1,2,0:T(2,128)S(1)} %fusion.101), channel_id=1, source_target_pairs={{0,1},{1,0},{2,3},{3,2},{4,5},{5,4},{6,7},{7,6},{8,9},{9,8},{10,11... | collective-permute-start | bytes 12296 | tf_op jit(solution)/shard_map/ppermute | solution.py:74
  43.8 1.4 %collective-permute-start.4 = (f32[]{:T(128)}, f32[]{:T(128)}, u32[]{:S(2)}, u32[]{:S(2)}) collective-permute-start(f32[]{:T(128)} %get-tuple-element.7), channel_id=1, source_target_pairs={{0,8},{8,0},{16,24},{24,16},{1,9},{9,1},{17,25},{25,17},{2,10},{10... | collective-permute-start | bytes 20 | tf_op jit(solution)/shard_map/ppermute | solution.py:74
  46.5 3.7 %collective-permute-start.5 = (f32[]{:T(128)}, f32[]{:T(128)}, u32[]{:S(2)}, u32[]{:S(2)}) collective-permute-start(f32[]{:T(128)} %add.201), channel_id=1, source_target_pairs={{0,16},{8,24},{16,0},{24,8},{1,17},{9,25},{17,1},{25,9},{2,18},{10... | collective-permute-start | bytes 20 | tf_op jit(solution)/shard_map/ppermute | solution.py:74
  50.9 3.7 %collective-permute-start.6 = (f32[]{:T(128)}, f32[]{:T(128)}, u32[]{:S(2)}, u32[]{:S(2)}) collective-permute-start(f32[]{:T(128)} %add.202), channel_id=1, source_target_pairs={{0,4},{4,0},{1,5},{5,1},{2,6},{6,2},{3,7},{7,3},{8,12},{12,8},{9,1... | collective-permute-start | bytes 20 | tf_op jit(solution)/shard_map/ppermute | solution.py:74
  55.2 3.7 %collective-permute-start.7 = (f32[]{:T(128)}, f32[]{:T(128)}, u32[]{:S(2)}, u32[]{:S(2)}) collective-permute-start(f32[]{:T(128)} %add.203), channel_id=1, source_target_pairs={{0,1},{1,0},{2,3},{3,2},{4,5},{5,4},{6,7},{7,6},{8,9},{9,8},{10,11... | collective-permute-start | bytes 20 | tf_op jit(solution)/shard_map/ppermute | solution.py:74
  59.6 4.6 %collective-permute-start.8 = (f32[]{:T(128)}, f32[]{:T(128)}, u32[]{:S(2)}, u32[]{:S(2)}) collective-permute-start(f32[]{:T(128)} %add.204), channel_id=1, source_target_pairs={{0,2},{1,3},{2,0},{3,1},{4,6},{5,7},{6,4},{7,5},{8,10},{9,11},{10,... | collective-permute-start | bytes 20 | tf_op jit(solution)/shard_map/ppermute | solution.py:74
  64.9 5.2 %copy-start.4 = (f32[16,32,128]{2,1,0:T(8,128)S(1)}, f32[16,32,128]{2,1,0:T(8,128)}, u32[]{:S(2)}) copy-start(f32[16,32,128]{2,1,0:T(8,128)} %param.10) | copy-start | bytes 786436
  65.0 5.2 %copy-start.1 = (f32[16,32,128]{2,1,0:T(8,128)S(1)}, f32[16,32,128]{2,1,0:T(8,128)}, u32[]{:S(2)}) copy-start(f32[16,32,128]{2,1,0:T(8,128)} %param.6) | copy-start | bytes 786436
  65.0 5.1 %copy-start.3 = (f32[16,32,128]{2,1,0:T(8,128)S(1)}, f32[16,32,128]{2,1,0:T(8,128)}, u32[]{:S(2)}) copy-start(f32[16,32,128]{2,1,0:T(8,128)} %param.11) | copy-start | bytes 786436
  65.0 4.9 %collective-permute-start.3 = (f32[16,32,4]{1,2,0:T(4,128)S(1)}, f32[16,32,4]{1,2,0:T(4,128)S(1)}, u32[]{:S(2)}, u32[]{:S(2)}) collective-permute-start(f32[16,32,4]{1,2,0:T(4,128)S(1)} %pad_maximum_fusion.1), channel_id=1, source_target_pairs={{0,2},{1,3},{2,0},{3,1},{4,6},{5,7},{6,4},{7,5},{8,10},{9,11},{10,... | collective-permute-start | bytes 24584 | tf_op jit(solution)/shard_map/ppermute | solution.py:74
  73.4 1.4 %collective-permute-start.9 = (f32[]{:T(128)}, f32[]{:T(128)}, u32[]{:S(2)}, u32[]{:S(2)}) collective-permute-start(f32[]{:T(128)} %get-tuple-element.4), channel_id=1, source_target_pairs={{0,8},{8,0},{16,24},{24,16},{1,9},{9,1},{17,25},{25,17},{2,10},{10... | collective-permute-start | bytes 20 | tf_op jit(solution)/shard_map/ppermute | solution.py:74
  76.1 3.7 %collective-permute-start.10 = (f32[]{:T(128)}, f32[]{:T(128)}, u32[]{:S(2)}, u32[]{:S(2)}) collective-permute-start(f32[]{:T(128)} %add.209), channel_id=1, source_target_pairs={{0,16},{8,24},{16,0},{24,8},{1,17},{9,25},{17,1},{25,9},{2,18},{10... | collective-permute-start | bytes 20 | tf_op jit(solution)/shard_map/ppermute | solution.py:74
  80.5 3.7 %collective-permute-start.11 = (f32[]{:T(128)}, f32[]{:T(128)}, u32[]{:S(2)}, u32[]{:S(2)}) collective-permute-start(f32[]{:T(128)} %add.210), channel_id=1, source_target_pairs={{0,4},{4,0},{1,5},{5,1},{2,6},{6,2},{3,7},{7,3},{8,12},{12,8},{9,1... | collective-permute-start | bytes 20 | tf_op jit(solution)/shard_map/ppermute | solution.py:74
  84.8 3.7 %collective-permute-start.12 = (f32[]{:T(128)}, f32[]{:T(128)}, u32[]{:S(2)}, u32[]{:S(2)}) collective-permute-start(f32[]{:T(128)} %add.211), channel_id=1, source_target_pairs={{0,1},{1,0},{2,3},{3,2},{4,5},{5,4},{6,7},{7,6},{8,9},{9,8},{10,11... | collective-permute-start | bytes 20 | tf_op jit(solution)/shard_map/ppermute | solution.py:74
  89.2 4.6 %collective-permute-start.13 = (f32[]{:T(128)}, f32[]{:T(128)}, u32[]{:S(2)}, u32[]{:S(2)}) collective-permute-start(f32[]{:T(128)} %add.212), channel_id=1, source_target_pairs={{0,2},{1,3},{2,0},{3,1},{4,6},{5,7},{6,4},{7,5},{8,10},{9,11},{10,... | collective-permute-start | bytes 20 | tf_op jit(solution)/shard_map/ppermute | solution.py:74
